TPU v7x, 32 devices: a whole 2x2x4 slice. The times are simulated.
32 devices in a mesh: rows: 16 (over z, y, x), cols: 2 (over core).
Axes of the slice: x: 2, y: 2, z: 4, core: 2. Of those that a mesh axis runs over, the one named last changes fastest.
Arguments:
- rhs: float32 [2, 96, 6144], P('cols', 'rows'), may hold values from -6 to 6
- pattern: int32 [48, 2], P(None, 'cols'), may hold values 0 or 1
- front_blocks: int32 [16, 4], replicated, may hold values from 0 to 47, as said below
- front_slot: int32 [16], replicated, may hold values from 0 to 31, as said below
- pivot_inverse: float32 [32, 256, 256], P('rows'), may hold values from -0.375 to 0.375
- update_factor: float32 [32, 256, 256], P('rows'), may hold values from -0.375 to 0.375
Outputs:
- solution: float32 [2, 96, 6144], P('cols', 'rows')
Inputs may be any that keep to these rules, and one draw needn't show every extreme that they name: `front_blocks`: columns 0 and 1 together name every row block that is no contribution block exactly once; columns 2 and 3 of a front are two different blocks, never a pivot block of any front. `front_slot`: all different; slot s belongs to index s // 2 of rows; some index holds 2 fronts in every draw; slots that no front names are unused.
All inputs are finite; a program needn't handle non-finite values. No bound on the sum of `pattern` on one device may be relied on, other than what follows from the above.
Results may differ from a plain program's by a relative error of at most 0.0001.
Values sent between devices are 32-bit elements; how exact they have to be, the bound alone decides.
A program may use at most 64 MiB of HBM per device.

v0:
```python
import functools

import jax
import jax.numpy as jnp
from jax import lax
from jax.experimental import pallas as pl
from jax.experimental.pallas import tpu as pltpu
from jax.sharding import PartitionSpec as P

BLOCK = 128
COLS = 6
PAIR = 2
PARTS = 8


def split(value):
    high = value.astype(jnp.bfloat16)
    low = (value - high.astype(jnp.float32)).astype(jnp.bfloat16)
    return high, low


def times(x, high, low, inner):
    dims = (((1,), (inner,)), ((), ()))
    x_high, x_low = split(x)
    dot = functools.partial(lax.dot_general, dimension_numbers=dims, preferred_element_type=jnp.float32)
    return dot(x_high, high) + (dot(x_low, high) + dot(x_high, low))


def kernel(
    n, fronts, blocks, chunk,
    rhs_hbm, pattern_hbm, fb_hbm, slot_hbm, inv_hbm, upd_hbm,
    out_ref,
    x, snd, rcv, back, pool, last, halves, inv, upd, wide, sep_rows, coef,
    pattern, fb, slot, front_of, place_of, src, sep,
    local_sem, out_send, out_recv, back_send, back_recv,
):
    me = lax.axis_index("rows")
    col = lax.axis_index("cols")
    slots = PAIR * n
    seps = blocks - 2 * fronts
    few = n <= 16

    def target(peer):
        return {"rows": peer, "cols": col}

    half = n // PARTS

    def offset(p):
        return PARTS * (p % half) + p // half

    def for_part(g, body):
        first = max(g * half, 1)
        if few:
            for p in sorted(range(first, (g + 1) * half), key=lambda p: -abs(offset(p) - n // 2)):
                body(p)
        else:
            def step(p, carry):
                body(p)
                return carry
            lax.fori_loop(first, (g + 1) * half, step, 0)

    def ahead(p):
        return lax.rem(me + offset(p), n)

    def behind(p):
        return lax.rem(me + n - offset(p), n)

    def repeat(count, body, unroll=1):
        def step(i, carry):
            body(i)
            return carry
        lax.fori_loop(0, count, step, 0, unroll=unroll if few else 1)

    pieces = [
        (rhs_hbm, x), (pattern_hbm, pattern), (fb_hbm, fb), (slot_hbm, slot), (inv_hbm, inv), (upd_hbm, upd),
    ]
    loads = [pltpu.make_async_copy(a, b, local_sem.at[i]) for i, (a, b) in enumerate(pieces)]
    for i in (3, 2, 1, 0):
        loads[i].start()

    barrier = pltpu.get_barrier_semaphore()
    for g in range(PARTS):
        for_part(g, lambda p: pl.semaphore_signal(
            barrier, inc=1, device_id=target(ahead(p)), device_id_type=pl.DeviceIdType.MESH
        ))
    for i in (4, 5):
        loads[i].start()

    def total(count, term):
        if few:
            values = [term(i) for i in range(count)]
            while len(values) > 1:
                pairs = [a + b for a, b in zip(values[::2], values[1::2])]
                values = pairs + ([values[-1]] if len(values) % 2 else [])
            return values[0]
        return lax.fori_loop(0, count, lambda i, t: t + term(i), 0)

    loads[3].wait()

    def find_front(s):
        front_of[s] = jnp.minimum(total(fronts, lambda f: jnp.where(slot[f] == s, f, 0)), fronts - 1)

    repeat(slots, find_front, 2)
    for i in (2, 1, 0):
        loads[i].wait()

    def block_rows(b, first, count):
        mask = pattern[b].astype(jnp.float32)
        return x[pl.ds(first * blocks + b, count, stride=blocks), :] * mask

    def pack(p):
        d = ahead(p)
        for k in range(PAIR):
            f = front_of[PAIR * d + k]
            b0, b1 = fb[0, f], fb[1, f]
            snd[k, p, 0] = block_rows(b0, 0, 4)
            snd[k, p, 1, 0:2, :] = block_rows(b0, 4, 2)
            snd[k, p, 1, 2:4, :] = block_rows(b1, 0, 2)
            snd[k, p, 2] = block_rows(b1, 2, 4)

    repeat(n, pack, 2)
    pl.semaphore_wait(barrier, n - 1)

    steps = [(k, g) for g in range(PARTS) for k in range(PAIR)]
    for i, (k, g) in enumerate(steps):
        for_part(g, lambda p, i=i, k=k: pltpu.make_async_remote_copy(
            src_ref=snd.at[k, p], dst_ref=rcv.at[k, p], send_sem=out_send.at[i], recv_sem=out_recv.at[i],
            device_id=target(ahead(p)), device_id_type=pl.DeviceIdType.MESH,
        ).start())
    for k in range(PAIR):
        rcv[k, 0] = snd[k, 0]

    loads[4].wait()
    loads[5].wait()
    width = inv.shape[1]
    strict = lax.broadcasted_iota(jnp.int32, (width, width), 0) > lax.broadcasted_iota(jnp.int32, (width, width), 1)
    for k in range(PAIR):
        high, low = split(jnp.where(strict, inv[k], 0.0))
        wide[k, 0, :width], wide[k, 1, :width] = high, low
        wide[k, 0, width:], wide[k, 1, width:] = split(upd[k] + times(upd[k], high, low, 0))
    halves[...] = jnp.zeros(halves.shape, jnp.float32)
    last[...] = jnp.zeros(last.shape, jnp.float32)

    def find_place(f):
        s = slot[f]
        away = lax.rem(lax.div(s, PAIR) + n - me, n)
        p = lax.rem(away, PARTS) * half + lax.div(away, PARTS)
        place_of[f] = 3 * (lax.rem(s, PAIR) * n + p) + 1

    repeat(fronts, find_place, 4)

    def find_source(b, rank):
        def term(f):
            at = place_of[f]
            return jnp.where(fb[0, f] == b, at, 0) + jnp.where(fb[1, f] == b, at + 1, 0)

        place = total(fronts, term)
        is_sep = place == 0
        src[b] = jnp.minimum(jnp.where(is_sep, 3 * slots + rank, place - 1), 3 * slots + seps - 1)
        return rank + jnp.where(is_sep, 1, 0)

    lax.fori_loop(0, blocks, find_source, 0)

    def landed(buffer, count, sem):
        view = buffer.at[pl.ds(0, count)]
        return pltpu.make_async_copy(view, view, sem)

    def flat(a):
        return a.reshape(8 * half, BLOCK)

    def remote(g):
        return half - 1 if g == 0 else half

    for i, (k, g) in enumerate(steps):
        landed(rcv.at[k], remote(g), out_recv.at[i]).wait()
        here = slice(g * half, (g + 1) * half)
        halves[i, 0, :, 0:4, :] = rcv[k, here, 0]
        halves[i, 0, :, 4:6, :] = rcv[k, here, 1, 0:2, :]
        halves[i, 1, :, 0:2, :] = rcv[k, here, 1, 2:4, :]
        halves[i, 1, :, 2:6, :] = rcv[k, here, 2]
        pivots = jnp.concatenate([flat(halves[i, 0]), flat(halves[i, 1])], axis=1)
        both = times(pivots, wide[k, 0], wide[k, 1], 1)
        solved = pivots + both[:, :width]
        update = both[:, width:]
        quads = [
            part.reshape(half, 8, BLOCK)
            for part in (solved[:, :BLOCK], solved[:, BLOCK:], update[:, :BLOCK], update[:, BLOCK:])
        ]
        for t in range(3):
            back[k, here, t, 0:6, :] = quads[t][:, 0:6]
            back[k, here, t, 6:8, :] = quads[3][:, 2 * t:2 * t + 2]

        for_part(g, lambda p, i=i, k=k: pltpu.make_async_remote_copy(
            src_ref=back.at[k, p], dst_ref=pool.at[pl.ds(3 * (k * n + p), 3)],
            send_sem=back_send.at[i], recv_sem=back_recv.at[i],
            device_id=target(behind(p)), device_id_type=pl.DeviceIdType.MESH,
        ).start())
        if g == 0:
            pool[3 * k * n:3 * k * n + 3] = back[k, 0]

    def find_separator(j):
        b = lax.fori_loop(
            0, blocks, lambda b, t: t + jnp.where(src[b] == 3 * slots + j, b, 0), 0, unroll=16 if few else 1
        )
        b = jnp.minimum(b, blocks - 1)
        sep[j] = b
        sep_rows[pl.ds(j, 1), :] = jnp.full((1, BLOCK), b, jnp.int32)
        pool[3 * slots + j, 0:6, :] = block_rows(b, 0, COLS)
        pool[3 * slots + j, 6:8, :] = jnp.zeros((2, BLOCK), jnp.float32)

    repeat(seps, find_separator)

    def weigh(g):
        rows = sep_rows[pl.ds(pl.multiple_of(g * chunk, chunk), chunk), :]

        def one_place(p):
            for k in range(PAIR):
                s = PAIR * ahead(p) + k
                f = front_of[s]
                used = slot[f] == s
                for h in range(2):
                    named = jnp.where(used, fb[2 + h, f], -1)
                    coef[(g * slots + k * n + p) * 2 + h] = jnp.where(rows == named, -1.0, 0.0)

        repeat(n, one_place, 4)

    repeat(seps // chunk, weigh)

    for i, (k, part) in enumerate(steps):
        landed(pool, 3 * remote(part), back_recv.at[i]).wait()
        begin = k * n + part * half
        for t in range(3):
            last[begin:begin + half, 2 * t:2 * t + 2, :] = pool[pl.ds(3 * begin + t, half, stride=3), 6:8, :]

        def add_up(g, begin=begin):
            first = 3 * slots + g * chunk

            def one_slot(o, accs):
                q = begin + o
                parts = (pool[3 * q + 2], last[q])
                for h in range(2):
                    row = (g * slots + q) * 2 + h
                    accs = tuple(a + coef[row, j:j + 1, :] * parts[h] for j, a in enumerate(accs))
                return accs

            accs = tuple(pool[first + j] for j in range(chunk))
            accs = lax.fori_loop(0, half, one_slot, accs, unroll=4 if few else 1)
            for j in range(chunk):
                pool[first + j] = accs[j]

        repeat(seps // chunk, add_up)

    def put(b):
        out_ref[pl.ds(b, COLS, stride=blocks), :] = pool[src[b], 0:6, :]

    repeat(blocks, put, 16)

    for i, (k, g) in enumerate(steps):
        landed(snd.at[k], remote(g), out_send.at[i]).wait()
        landed(back.at[k], remote(g), back_send.at[i]).wait()


def on_device(n, rhs, pattern, front_blocks, front_slot, pivot_inverse, update_factor):
    fronts = front_blocks.shape[0]
    columns, total_rows = rhs.shape[1:]
    blocks = total_rows // BLOCK
    assert columns == COLS and pivot_inverse.shape[0] == PAIR
    width = pivot_inverse.shape[1]
    slots = PAIR * n
    seps = blocks - 2 * fronts
    f32, i32 = jnp.float32, jnp.int32
    chunk = next(c for c in (16, 8, 4, 2, 1) if seps % c == 0)
    result = pl.pallas_call(
        functools.partial(kernel, n, fronts, blocks, chunk),
        out_shape=pltpu.VMEM((columns * blocks, BLOCK), f32),
        in_specs=[pl.BlockSpec(memory_space=pl.ANY)] * 6,
        out_specs=pl.BlockSpec(memory_space=pltpu.VMEM),
        scratch_shapes=[
            pltpu.VMEM((columns * blocks, BLOCK), f32),
            pltpu.VMEM((PAIR, n, 3, 4, BLOCK), f32),
            pltpu.VMEM((PAIR, n, 3, 4, BLOCK), f32),
            pltpu.VMEM((PAIR, n, 3, 8, BLOCK), f32),
            pltpu.VMEM((3 * slots + seps, 8, BLOCK), f32),
            pltpu.VMEM((slots, 8, BLOCK), f32),
            pltpu.VMEM((PAIR * PARTS, 2, n // PARTS, 8, BLOCK), f32),
            pltpu.VMEM((PAIR, width, width), f32),
            pltpu.VMEM((PAIR, width, width), f32),
            pltpu.VMEM((PAIR, 2, 2 * width, width), jnp.bfloat16),
            pltpu.VMEM((seps, BLOCK), i32),
            pltpu.VMEM((seps // chunk * slots * 2, chunk, BLOCK), f32),
            pltpu.SMEM((blocks,), i32),
            pltpu.SMEM((4, fronts), i32),
            pltpu.SMEM((fronts,), i32),
            pltpu.SMEM((slots,), i32),
            pltpu.SMEM((fronts,), i32),
            pltpu.SMEM((blocks,), i32),
            pltpu.SMEM((seps,), i32),
            pltpu.SemaphoreType.DMA((6,)),
            pltpu.SemaphoreType.DMA((PAIR * PARTS,)),
            pltpu.SemaphoreType.DMA((PAIR * PARTS,)),
            pltpu.SemaphoreType.DMA((PAIR * PARTS,)),
            pltpu.SemaphoreType.DMA((PAIR * PARTS,)),
        ],
        compiler_params=pltpu.CompilerParams(collective_id=0, has_side_effects=True),
    )(
        rhs.reshape(columns * blocks, BLOCK),
        pattern.reshape(-1),
        front_blocks.T,
        front_slot,
        pivot_inverse,
        update_factor,
    )
    return result.reshape(1, columns, total_rows)


def solution(mesh):
    return jax.shard_map(
        functools.partial(on_device, mesh.shape["rows"]),
        mesh=mesh,
        in_specs=(
            P("cols", "rows", None),
            P(None, "cols"),
            P(),
            P(),
            P("rows", None, None),
            P("rows", None, None),
        ),
        out_specs=P("cols", "rows", None),
        check_vma=False,
    )
```

profile of v0, /device:TPU:0, one launch (start us, length us, event | category | flops | bytes accessed | tf_op | source)
XLA Modules:
  0.0 21.7 jit_solution(2793007568326498553)
XLA Ops:
  0.0 21.0 %shard_map.64 = f32[288,128]{1,0:T(8,128)S(1)} custom-call(f32[288,128]{1,0:T(8,128)} %bitcast.5, s32[48]{0:T(128)} %bitcast.7, s32[4,16]{1,0:T(4,128)} %bitcast.6, s32[16]{0:T(128)} %slot_hbm.1, f32[2,256,256]{2,1,0:T(8,128)} %inv_hbm.1, f32[2,256,256]{2,1,0:T(8,128)} %upd_hbm.1), custom_call_target="tpu_custom_call" | custom-call | tf_op jit(solution)/shard_map/pallas_call | solution.py:273
  21.0 0.7 %copy.10 = f32[1,6,6144]{2,0,1:T(1,128)} copy(f32[1,6,6144]{2,0,1:T(1,128)S(1)} %bitcast.4) | data formatting | bytes 294912
where the time goes:
time: 21.8 us; the launch traced here: 21.7 us
  Pallas kernels  21 us (96%)
  local copies, waits for them, and re-layouts  0.66 us (3%)
    pallas_call x1, Pallas kernels, on_device(): pl.pallas_call(functools.partial(kernel, n, fronts, blocks, chunk), out_s...  21 us
    unnamed x1, local copies, waits for them, and re-layouts  0.66 us

commit v1 on v0

v1 whole, which is shorter than its diff:
```python
import functools

import jax
import jax.numpy as jnp
from jax import lax
from jax.experimental import pallas as pl
from jax.experimental.pallas import tpu as pltpu
from jax.sharding import PartitionSpec as P

BLOCK = 128
COLS = 6
PAIR = 2
PARTS = 8
MESH = pl.DeviceIdType.MESH
WORK = ((0, 1), (2, 3), (6, 7), (4, 5))
GATHER = (0, 1, 2, 3, 6, 7, 4, 5)
OUT = (0, 1, 2, 3, 6, 7, 4, 5)
ROOT = (7, 6, 5, 4, 3, 2, 1, 0)


def split(value):
    high = value.astype(jnp.bfloat16)
    low = (value - high.astype(jnp.float32)).astype(jnp.bfloat16)
    return high, low


def times(x, high, low, inner):
    dims = (((1,), (inner,)), ((), ()))
    x_high, x_low = split(x)
    rows = x.shape[0]
    dot = functools.partial(lax.dot_general, dimension_numbers=dims, preferred_element_type=jnp.float32)
    both = dot(jnp.concatenate([x_high, x_low], axis=0), high)
    return both[:rows] + (both[rows:] + dot(x_high, low))


def kernel(
    n, fronts, blocks, chunk,
    rhs_hbm, pattern_hbm, fb_hbm, slot_hbm, row_hbm, inv_hbm, upd_hbm,
    out_ref,
    x, snd, rcv, back, pool, last, halves, inv, upd, wide, coef, fbv, slotv, table,
    pattern, fb, slot, front_of, src,
    local_sem, out_send, out_recv, back_send, back_recv, root_sem,
):
    me = lax.axis_index("rows")
    col = lax.axis_index("cols")
    slots = PAIR * n
    seps = blocks - 2 * fronts
    first = 6 * n
    few = n <= 16
    per = n // PARTS

    def offset(p):
        return PARTS * (p % per) + p // per

    def ahead(p):
        return lax.rem(me + offset(p), n)

    def behind(p):
        return lax.rem(me + n - offset(p), n)

    def place_of(away):
        return lax.rem(away, PARTS) * per + lax.div(away, PARTS)

    def device(index, core=col):
        return {"rows": index, "cols": core}

    lead, root = col == 1, jnp.logical_and(me == 0, col == 0)
    plain = jnp.logical_and(me != 0, col == 0)
    skipped = jnp.where(plain, place_of(me), -1)

    def span(begin, end, body):
        if few:
            for p in range(begin, end):
                body(p)
        else:
            def step(p, carry):
                body(p)
                return carry
            lax.fori_loop(begin, end, step, 0)

    def repeat(count, body, unroll=1):
        def step(i, carry):
            body(i)
            return carry
        lax.fori_loop(0, count, step, 0, unroll=unroll if few else 1)

    pieces = [
        (rhs_hbm, x), (pattern_hbm, pattern), (fb_hbm, fb), (slot_hbm, slot), (inv_hbm, inv), (upd_hbm, upd),
        (fb_hbm, fbv), (row_hbm, slotv),
    ]
    loads = [pltpu.make_async_copy(a, b, local_sem.at[i]) for i, (a, b) in enumerate(pieces)]
    for i in (3, 2, 1, 0):
        loads[i].start()

    barrier = pltpu.get_barrier_semaphore()

    def greet(p, core=col):
        pl.semaphore_signal(barrier, inc=1, device_id=device(ahead(p), core), device_id_type=MESH)

    span(1, n, lambda p: pl.when(jnp.logical_not(jnp.logical_and(col == 0, ahead(p) == 0)))(lambda: greet(p)))
    pl.when(lead)(lambda: pl.semaphore_signal(barrier, inc=1, device_id=device(0, 0), device_id_type=MESH))
    for i in (6, 7, 4, 5):
        loads[i].start()

    def total(count, term):
        if few:
            values = [term(i) for i in range(count)]
            while len(values) > 1:
                pairs = [a + b for a, b in zip(values[::2], values[1::2])]
                values = pairs + ([values[-1]] if len(values) % 2 else [])
            return values[0]
        return lax.fori_loop(0, count, lambda i, t: t + term(i), 0)

    loads[3].wait()

    def find_front(s):
        front_of[s] = jnp.minimum(total(fronts, lambda f: jnp.where(slot[f] == s, f, 0)), fronts - 1)

    repeat(slots, find_front, 2)
    for i in (2, 1, 0):
        loads[i].wait()

    def rows_of(b):
        return pl.ds(b, COLS, stride=blocks)

    def mask(b):
        x[rows_of(b), :] = x[rows_of(b), :] * pattern[b].astype(jnp.float32)

    repeat(blocks, mask, 16)

    def part(b, begin, count):
        return x[pl.ds(begin * blocks + b, count, stride=blocks), :]

    def pack(p):
        d = ahead(p)
        for k in range(PAIR):
            f = front_of[PAIR * d + k]
            b0, b1 = fb[0, f], fb[1, f]
            snd[p, k, 0] = part(b0, 0, 4)
            snd[p, k, 1, 0:2, :] = part(b0, 4, 2)
            snd[p, k, 1, 2:4, :] = part(b1, 0, 2)
            snd[p, k, 2] = part(b1, 2, 4)

    repeat(n, pack, 2)
    def fill(buffer, p):
        buffer[p] = snd[0]

    rcv[0] = snd[0]
    pl.when(col == 0)(lambda: fill(rcv, n))
    pl.when(plain)(lambda: fill(rcv, place_of(me)))

    def group(p):
        return p // per if isinstance(p, int) else lax.div(p, per)

    def send_out(p):
        pltpu.make_async_remote_copy(
            src_ref=snd.at[p], dst_ref=rcv.at[p], send_sem=out_send.at[group(p)], recv_sem=out_recv.at[group(p)],
            device_id=device(ahead(p)), device_id_type=MESH,
        ).start()

    def send_root(p):
        pltpu.make_async_remote_copy(
            src_ref=snd.at[p], dst_ref=rcv.at[n], send_sem=out_send.at[group(p)], recv_sem=root_sem.at[0],
            device_id=device(ahead(p), 1), device_id_type=MESH,
        ).start()

    pl.semaphore_wait(barrier, jnp.where(root, n, n - 1))

    @pl.when(jnp.logical_not(root))
    def _():
        for g in OUT:
            span(max(g * per, 1), (g + 1) * per, send_out)

    @pl.when(root)
    def _():
        for g in ROOT:
            span(g * per, (g + 1) * per, send_root)

    width = inv.shape[1]

    def widen():
        for i in (4, 5):
            loads[i].wait()
        row = lax.broadcasted_iota(jnp.int32, (width, width), 0)
        strict = row > lax.broadcasted_iota(jnp.int32, (width, width), 1)
        for k in range(PAIR):
            high, low = split(jnp.where(strict, inv[k], 0.0))
            wide[k, 0, :width], wide[k, 1, :width] = high, low
            wide[k, 0, width:], wide[k, 1, width:] = split(upd[k] + times(upd[k], high, low, 0))
        halves[...] = jnp.zeros(halves.shape, jnp.float32)

    tell = pltpu.make_async_copy(table, src, local_sem.at[8])

    def find_sources():
        for i in (6, 7):
            loads[i].wait()
        last[...] = jnp.zeros(last.shape, jnp.float32)
        pool[first:] = jnp.zeros((seps, 8, BLOCK), jnp.float32)

        owner = lax.div(slotv[...], PAIR)
        away = lax.rem(owner + n - me, n)
        position = lax.rem(away, PARTS) * per + lax.div(away, PARTS)
        place = 6 * position + 3 * lax.rem(slotv[...], PAIR)
        block = lax.broadcasted_iota(jnp.int32, (blocks, fronts), 0)
        value = jnp.zeros((blocks, fronts), jnp.int32)
        for h in range(2):
            named = fbv[h:h + 1, :]
            value = value + jnp.where(named == block, place + (h + 1), 0) + jnp.where(named < block, 4096, 0)
        value = jnp.sum(value.astype(jnp.float32), axis=1, keepdims=True).astype(jnp.int32)
        at, before = lax.rem(value, 4096), lax.div(value, 4096)
        own = lax.broadcasted_iota(jnp.int32, (blocks, 1), 0)
        found = jnp.where(at == 0, first + own - before, at - 1)
        lanes = table.shape[1]
        turned = jnp.where(
            lax.broadcasted_iota(jnp.int32, (blocks, lanes), 0) == lax.broadcasted_iota(jnp.int32, (blocks, lanes), 1),
            found, 0,
        )
        table[...] = jnp.sum(turned.astype(jnp.float32), axis=0, keepdims=True).astype(jnp.int32)
        tell.start()

    def landed(buffer, count, sem):
        view = buffer.at[pl.ds(0, count)]
        return pltpu.make_async_copy(view, view, sem)

    widen()
    find_sources()

    def remote(g):
        return per - 1 if isinstance(g, int) and g == 0 else per

    def source(b):
        return jnp.clip(src[0, b], 0, first + seps - 1)

    def weigh(c):
        rows = c * chunk + lax.broadcasted_iota(jnp.int32, (chunk, BLOCK), 0)

        def one_place(p):
            d = ahead(p)
            for k in range(PAIR):
                s = PAIR * d + k
                f = front_of[s]
                used = slot[f] == s
                for h in range(2):
                    named = jnp.where(used, source(fb[2 + h, f]) - first, -1)
                    coef[((c * n + p) * PAIR + k) * 2 + h] = jnp.where(rows == named, -1.0, 0.0)

        repeat(n, one_place, 4)

    def begin_with(b):
        keep = jnp.where(source(b) >= first, 1.0, 0.0)
        out_ref[rows_of(b), :] = x[rows_of(b), :] * keep

    def prepare():
        tell.wait()
        repeat(seps // chunk, weigh)
        repeat(blocks, begin_with, 16)

    def less(g, wait):
        none = jnp.logical_and(plain, lax.rem(me, PARTS) == g)
        if g > 0 or per > 2:
            pl.when(none)(lambda: wait(remote(g) - 1))
        pl.when(jnp.logical_not(none))(lambda: wait(remote(g)))

    def more(g, wait):
        if g > 0:
            wait(remote(g))
        else:
            pl.when(root)(lambda: wait(per))
            pl.when(jnp.logical_not(root))(lambda: wait(remote(g)))

    def work(i, names):
        parts = list(names)
        for g in parts:
            less(g, lambda count: landed(rcv, count, out_recv.at[g]).wait())
        count = len(parts) * per
        if parts[-1] == PARTS - 1:
            count += 1
            pl.when(lead)(lambda: landed(rcv, 1, root_sem.at[0]).wait())
        here = pl.ds(parts[0] * per, count)
        for k in range(PAIR):
            half = halves.at[PAIR * i + k]
            half[0, 0:count, 0:4, :] = rcv[here, k, 0]
            half[0, 0:count, 4:6, :] = rcv[here, k, 1, 0:2, :]
            half[1, 0:count, 0:2, :] = rcv[here, k, 1, 2:4, :]
            half[1, 0:count, 2:6, :] = rcv[here, k, 2]
            flat = [half[h, 0:count].reshape(8 * count, BLOCK) for h in range(2)]
            pivots = jnp.concatenate(flat, axis=1)
            both = times(pivots, wide[k, 0], wide[k, 1], 1)
            solved = pivots + both[:, :width]
            update = both[:, width:]
            quads = [
                part.reshape(count, 8, BLOCK)
                for part in (solved[:, :BLOCK], solved[:, BLOCK:], update[:, :BLOCK], update[:, BLOCK:])
            ]
            for t in range(3):
                back[here, 3 * k + t, 0:6, :] = quads[t][:, 0:6]
                back[here, 3 * k + t, 6:8, :] = quads[3][:, 2 * t:2 * t + 2]
        if parts[-1] == PARTS - 1:
            pl.when(lead)(send_to_root.start)
        for g in parts:
            send_back(g)

    def send_back(g):
        def one(p):
            pl.when(p != skipped)(lambda: pltpu.make_async_remote_copy(
                src_ref=back.at[p], dst_ref=pool.at[pl.ds(6 * p, 6)], send_sem=back_send.at[g], recv_sem=back_recv.at[g],
                device_id=device(behind(p)), device_id_type=MESH,
            ).start())

        span(max(g * per, 1), (g + 1) * per, one)
        if g == 0:
            pl.when(jnp.logical_not(root))(keep)

    send_to_root = pltpu.make_async_remote_copy(
        src_ref=back.at[n], dst_ref=pool.at[pl.ds(6 * place_of(me), 6)],
        send_sem=root_sem.at[1], recv_sem=back_recv.at[lax.rem(me, PARTS)],
        device_id=device(0, 0), device_id_type=MESH,
    )

    def keep():
        pool[0:6] = back[0]

    for i, names in enumerate(WORK):
        work(i, names)

    prepare()

    def gather(g):
        more(g, lambda count: landed(pool, 6 * count, back_recv.at[g]).wait())
        begin = PAIR * g * per
        for t in range(3):
            tiles = pool[pl.ds(3 * begin + t, PAIR * per, stride=3), 6:8, :]
            last[pl.ds(begin, PAIR * per), 2 * t:2 * t + 2, :] = tiles

        def add_up(c):
            def one_slot(o, accs):
                q = begin + o
                parts = (pool[3 * q + 2], last[q])
                for h in range(2):
                    row = (c * slots + q) * 2 + h
                    accs = tuple(a + coef[row, j:j + 1, :] * parts[h] for j, a in enumerate(accs))
                return accs

            at = first + c * chunk
            accs = tuple(pool[at + j] for j in range(chunk))
            accs = lax.fori_loop(0, PAIR * per, one_slot, accs, unroll=4 if few else 1)
            for j in range(chunk):
                pool[at + j] = accs[j]

        repeat(seps // chunk, add_up)

    for g in GATHER:
        gather(g)

    def put(b):
        out_ref[rows_of(b), :] = out_ref[rows_of(b), :] + pool[source(b), 0:6, :]

    repeat(blocks, put, 16)

    for g in range(PARTS):
        more(g, lambda count: landed(snd, count, out_send.at[g]).wait())
        less(g, lambda count: landed(back, count, back_send.at[g]).wait())
    pl.when(lead)(send_to_root.wait_send)


def on_device(n, rhs, pattern, front_blocks, front_slot, pivot_inverse, update_factor):
    fronts = front_blocks.shape[0]
    columns, total_rows = rhs.shape[1:]
    blocks = total_rows // BLOCK
    assert columns == COLS and pivot_inverse.shape[0] == PAIR and n & (n - 1) == 0 and n >= 16
    width = pivot_inverse.shape[1]
    slots = PAIR * n
    seps = blocks - 2 * fronts
    f32, i32 = jnp.float32, jnp.int32
    chunk = next(c for c in (16, 8, 4, 2, 1) if seps % c == 0)
    lanes = pl.cdiv(blocks, BLOCK) * BLOCK
    dma = pltpu.SemaphoreType.DMA
    result = pl.pallas_call(
        functools.partial(kernel, n, fronts, blocks, chunk),
        out_shape=pltpu.VMEM((columns * blocks, BLOCK), f32),
        in_specs=[pl.BlockSpec(memory_space=pl.ANY)] * 7,
        out_specs=pl.BlockSpec(memory_space=pltpu.VMEM),
        scratch_shapes=[
            pltpu.VMEM((columns * blocks, BLOCK), f32),
            pltpu.VMEM((n, PAIR, 3, 4, BLOCK), f32),
            pltpu.VMEM((n + 1, PAIR, 3, 4, BLOCK), f32),
            pltpu.VMEM((n + 1, 6, 8, BLOCK), f32),
            pltpu.VMEM((6 * n + seps, 8, BLOCK), f32),
            pltpu.VMEM((slots, 8, BLOCK), f32),
            pltpu.VMEM((PAIR * len(WORK), 2, 2 * n // PARTS + 1, 8, BLOCK), f32),
            pltpu.VMEM((PAIR, width, width), f32),
            pltpu.VMEM((PAIR, width, width), f32),
            pltpu.VMEM((PAIR, 2, 2 * width, width), jnp.bfloat16),
            pltpu.VMEM((seps // chunk * slots * 2, chunk, BLOCK), f32),
            pltpu.VMEM((4, fronts), i32),
            pltpu.VMEM((1, fronts), i32),
            pltpu.VMEM((1, lanes), i32),
            pltpu.SMEM((blocks,), i32),
            pltpu.SMEM((4, fronts), i32),
            pltpu.SMEM((fronts,), i32),
            pltpu.SMEM((slots,), i32),
            pltpu.SMEM((1, lanes), i32),
            dma((9,)),
            dma((PARTS,)),
            dma((PARTS,)),
            dma((PARTS,)),
            dma((PARTS,)),
            dma((2,)),
        ],
        compiler_params=pltpu.CompilerParams(collective_id=0, has_side_effects=True),
    )(
        rhs.reshape(columns * blocks, BLOCK),
        pattern.reshape(-1),
        front_blocks.T,
        front_slot,
        front_slot.reshape(1, -1),
        pivot_inverse,
        update_factor,
    )
    return result.reshape(1, columns, total_rows)


def solution(mesh):
    return jax.shard_map(
        functools.partial(on_device, mesh.shape["rows"]),
        mesh=mesh,
        in_specs=(
            P("cols", "rows", None),
            P(None, "cols"),
            P(),
            P(),
            P("rows", None, None),
            P("rows", None, None),
        ),
        out_specs=P("cols", "rows", None),
        check_vma=False,
    )
```

time: 21.8 us -> 20.8 us (0.954)
  the two profiles are of different devices: /device:TPU:0 before, /device:TPU:4 now
where the time goes in v1:
time: 20.8 us; the launch traced here: 20.4 us
  Pallas kernels  19.8 us (95%)
  local copies, waits for them, and re-layouts  0.66 us (3%)
    pallas_call x1, Pallas kernels, on_device(): pl.pallas_call(functools.partial(kernel, n, fronts, blocks, chunk), out_s...  19.8 us
    unnamed x1, local copies, waits for them, and re-layouts  0.66 us

profile of v1, /device:TPU:4, one launch (start us, length us, event | category | flops | bytes accessed | tf_op | source)
XLA Modules:
  0.0 20.4 jit_solution(15003290573723087057)
XLA Ops:
  0.0 19.8 %shard_map.64 = f32[288,128]{1,0:T(8,128)S(1)} custom-call(f32[288,128]{1,0:T(8,128)} %bitcast.6, s32[48]{0:T(128)} %bitcast.9, s32[4,16]{1,0:T(4,128)} %bitcast.7, s32[16]{0:T(128)} %slot_hbm.1, s32[1,16]{1,0:T(1,128)} %bitcast.8, f32[2,256,256]{2,1,0:T(8,128)} %inv_hbm.1, f32[2,256,256]{2,1,0:T(8,128)} %upd_hbm.1), custom_call_target="tpu_custom_call" | custom-call | tf_op jit(solution)/shard_map/pallas_call | solution.py:378
  19.8 0.7 %copy.10 = f32[1,6,6144]{2,0,1:T(1,128)} copy(f32[1,6,6144]{2,0,1:T(1,128)S(1)} %bitcast.5) | data formatting | bytes 294912

commit v2 on v1

--- a/solution.py
+++ b/solution.py
@@ -15,7 +15,7 @@
 WORK = ((0, 1), (2, 3), (6, 7), (4, 5))
 GATHER = (0, 1, 2, 3, 6, 7, 4, 5)
 OUT = (0, 1, 2, 3, 6, 7, 4, 5)
-ROOT = (7, 6, 5, 4, 3, 2, 1, 0)
+ROOT = (1, 0, 2, 3, 7, 6, 5, 4)
 
 
 def split(value):
@@ -89,8 +89,7 @@
         (fb_hbm, fbv), (row_hbm, slotv),
     ]
     loads = [pltpu.make_async_copy(a, b, local_sem.at[i]) for i, (a, b) in enumerate(pieces)]
-    for i in (3, 2, 1, 0):
-        loads[i].start()
+    loads[3].start()
 
     barrier = pltpu.get_barrier_semaphore()
 
@@ -99,7 +98,7 @@
 
     span(1, n, lambda p: pl.when(jnp.logical_not(jnp.logical_and(col == 0, ahead(p) == 0)))(lambda: greet(p)))
     pl.when(lead)(lambda: pl.semaphore_signal(barrier, inc=1, device_id=device(0, 0), device_id_type=MESH))
-    for i in (6, 7, 4, 5):
+    for i in (0, 2, 1, 6, 7, 4, 5):
         loads[i].start()
 
     def total(count, term):
@@ -154,13 +153,13 @@
 
     def send_out(p):
         pltpu.make_async_remote_copy(
-            src_ref=snd.at[p], dst_ref=rcv.at[p], send_sem=out_send.at[group(p)], recv_sem=out_recv.at[group(p)],
+            src_ref=snd.at[p], dst_ref=rcv.at[p], send_sem=out_send.at[0], recv_sem=out_recv.at[group(p)],
             device_id=device(ahead(p)), device_id_type=MESH,
         ).start()
 
     def send_root(p):
         pltpu.make_async_remote_copy(
-            src_ref=snd.at[p], dst_ref=rcv.at[n], send_sem=out_send.at[group(p)], recv_sem=root_sem.at[0],
+            src_ref=snd.at[p], dst_ref=rcv.at[n], send_sem=out_send.at[0], recv_sem=root_sem.at[0],
             device_id=device(ahead(p), 1), device_id_type=MESH,
         ).start()
 
@@ -297,18 +296,19 @@
                 back[here, 3 * k + t, 6:8, :] = quads[3][:, 2 * t:2 * t + 2]
         if parts[-1] == PARTS - 1:
             pl.when(lead)(send_to_root.start)
-        for g in parts:
-            send_back(g)
-
-    def send_back(g):
+        for turn in range(2):
+            for g in parts:
+                send_back(g, turn)
+
+    def send_back(g, turn):
         def one(p):
-            pl.when(p != skipped)(lambda: pltpu.make_async_remote_copy(
-                src_ref=back.at[p], dst_ref=pool.at[pl.ds(6 * p, 6)], send_sem=back_send.at[g], recv_sem=back_recv.at[g],
+            pl.when(jnp.logical_and(p != skipped, (behind(p) < n // 4) == (turn == 0)))(lambda: pltpu.make_async_remote_copy(
+                src_ref=back.at[p], dst_ref=pool.at[pl.ds(6 * p, 6)], send_sem=back_send.at[0], recv_sem=back_recv.at[g],
                 device_id=device(behind(p)), device_id_type=MESH,
             ).start())
 
         span(max(g * per, 1), (g + 1) * per, one)
-        if g == 0:
+        if g == 0 and turn == 0:
             pl.when(jnp.logical_not(root))(keep)
 
     send_to_root = pltpu.make_async_remote_copy(
@@ -357,9 +357,10 @@
 
     repeat(blocks, put, 16)
 
-    for g in range(PARTS):
-        more(g, lambda count: landed(snd, count, out_send.at[g]).wait())
-        less(g, lambda count: landed(back, count, back_send.at[g]).wait())
+    pl.when(root)(lambda: landed(snd, n, out_send.at[0]).wait())
+    pl.when(jnp.logical_not(root))(lambda: landed(snd, n - 1, out_send.at[0]).wait())
+    pl.when(plain)(lambda: landed(back, n - 2, back_send.at[0]).wait())
+    pl.when(jnp.logical_not(plain))(lambda: landed(back, n - 1, back_send.at[0]).wait())
     pl.when(lead)(send_to_root.wait_send)
 
 

time: 20.8 us -> 20.4 us (0.981); the launches traced: 20.4 us -> 20.3 us
  no operation moved by 1% of the time
where the time goes in v2:
time: 20.4 us; the launch traced here: 20.3 us
  Pallas kernels  19.6 us (96%)
  local copies, waits for them, and re-layouts  0.66 us (3%)
    pallas_call x1, Pallas kernels, on_device(): pl.pallas_call(functools.partial(kernel, n, fronts, blocks, chunk), out_s...  19.6 us
    unnamed x1, local copies, waits for them, and re-layouts  0.66 us

profile of v2, /device:TPU:4, one launch (start us, length us, event | category | flops | bytes accessed | tf_op | source)
XLA Modules:
  0.0 20.3 jit_solution(1574604787050915664)
XLA Ops:
  0.0 19.6 %shard_map.64 = f32[288,128]{1,0:T(8,128)S(1)} custom-call(f32[288,128]{1,0:T(8,128)} %bitcast.6, s32[48]{0:T(128)} %bitcast.9, s32[4,16]{1,0:T(4,128)} %bitcast.7, s32[16]{0:T(128)} %slot_hbm.1, s32[1,16]{1,0:T(1,128)} %bitcast.8, f32[2,256,256]{2,1,0:T(8,128)} %inv_hbm.1, f32[2,256,256]{2,1,0:T(8,128)} %upd_hbm.1), custom_call_target="tpu_custom_call" | custom-call | tf_op jit(solution)/shard_map/pallas_call | solution.py:379
  19.6 0.7 %copy.10 = f32[1,6,6144]{2,0,1:T(1,128)} copy(f32[1,6,6144]{2,0,1:T(1,128)S(1)} %bitcast.5) | data formatting | bytes 294912

commit v3 on v2

--- a/solution.py
+++ b/solution.py
@@ -14,7 +14,7 @@
 MESH = pl.DeviceIdType.MESH
 WORK = ((0, 1), (2, 3), (6, 7), (4, 5))
 GATHER = (0, 1, 2, 3, 6, 7, 4, 5)
-OUT = (0, 1, 2, 3, 6, 7, 4, 5)
+OUT = (1, 0, 2, 3, 6, 7, 4, 5)
 ROOT = (1, 0, 2, 3, 7, 6, 5, 4)
 
 

time: 20.4 us -> 20.3 us (level)
  no operation moved by 1% of the time
where the time goes in v3:
time: 20.3 us; the launch traced here: 20.1 us
  Pallas kernels  19.5 us (96%)
  local copies, waits for them, and re-layouts  0.66 us (3%)
    pallas_call x1, Pallas kernels, on_device(): pl.pallas_call(functools.partial(kernel, n, fronts, blocks, chunk), out_s...  19.5 us
    unnamed x1, local copies, waits for them, and re-layouts  0.66 us

profile of v3, /device:TPU:4, one launch (start us, length us, event | category | flops | bytes accessed | tf_op | source)
XLA Modules:
  0.0 20.1 jit_solution(9477942558208205357)
XLA Ops:
  0.0 19.5 %shard_map.64 = f32[288,128]{1,0:T(8,128)S(1)} custom-call(f32[288,128]{1,0:T(8,128)} %bitcast.6, s32[48]{0:T(128)} %bitcast.9, s32[4,16]{1,0:T(4,128)} %bitcast.7, s32[16]{0:T(128)} %slot_hbm.1, s32[1,16]{1,0:T(1,128)} %bitcast.8, f32[2,256,256]{2,1,0:T(8,128)} %inv_hbm.1, f32[2,256,256]{2,1,0:T(8,128)} %upd_hbm.1), custom_call_target="tpu_custom_call" | custom-call | tf_op jit(solution)/shard_map/pallas_call | solution.py:379
  19.5 0.7 %copy.10 = f32[1,6,6144]{2,0,1:T(1,128)} copy(f32[1,6,6144]{2,0,1:T(1,128)S(1)} %bitcast.5) | data formatting | bytes 294912
